TPU v7x, 32 devices: a whole 2x2x4 slice. The times are simulated.
32 devices in a mesh: pb: 4 (over z), freq: 4 (over y, core), ga: 2 (over x).
Axes of the slice: x: 2, y: 2, z: 4, core: 2. Of those that a mesh axis runs over, the one named last changes fastest.
Arguments:
- densities: bfloat16 [4, 2, 256, 4096], P('pb', None, ('freq', 'ga')), may hold values from -0.5 to 0.5
- screened: bfloat16 [4, 4, 2, 4096, 4096], P('pb', 'freq', None, 'ga'), may hold values from -0.09375 to 0.09375
- energies: float32 [16, 256], replicated, may hold values from -2.5 to 2.5
- occupied: int32 [16], replicated, may hold values from 64 to 192
- kmq: int32 [4], replicated, may hold values from 0 to 15
- offsets: int32 [4], replicated, may hold values from -16 to 15
- weights: float32 [4], replicated, may hold values from 0.5 to 2
Outputs:
- sigma: float32 [2, 1, 64], P(None, None, ('pb', 'freq'))
All inputs are finite; a program needn't handle non-finite values.
Results may differ from a plain program's by a relative error of at most 0.0003.
Values may be sent and summed in bfloat16 or wider, within the bound.
A program may use at most 64 MiB of HBM per device.

v0:
```python
import functools
import math

import jax
import jax.numpy as jnp
from jax import lax
from jax.experimental import pallas as pl
from jax.experimental.pallas import tpu as pltpu
from jax.sharding import PartitionSpec as P

MESH = pl.DeviceIdType.MESH
CHUNKS = 8
TILE = 2048
AHEAD = 4

NB = 256
NS = 1
OUT_DEV = 4


broadening = 0.15


def from_behind(block, axis, distance):
    devices = range(lax.axis_size(axis))
    route = [((i - distance) % len(devices), i) for i in devices]
    return lax.ppermute(block, axis, route)


def green_parts(level_row, filled, freq_shift, omegas):
    bands = jnp.arange(level_row.shape[0], dtype=jnp.int32)
    pole_sign = jnp.where(bands < filled, -1.0, 1.0).astype(jnp.float32)
    real_part = omegas[None, :] - freq_shift - level_row[:, None]
    imag_part = broadening * pole_sign[:, None]
    denominator = real_part * real_part + imag_part * imag_part
    return (real_part / denominator, -imag_part / denominator)


def spectrum(pair_real, pair_imag, green_real, green_imag):
    exact = lax.Precision.HIGHEST
    real_out = jnp.dot(pair_real, green_real, precision=exact) - jnp.dot(
        pair_imag, green_imag, precision=exact
    )
    imag_out = jnp.dot(pair_real, green_imag, precision=exact) + jnp.dot(
        pair_imag, green_real, precision=exact
    )
    return jnp.stack([real_out, imag_out])


def panel_product(density_all, screen):
    pair_rows = density_all.shape[1]
    panel_rows = screen.shape[1]
    product = lax.dot_general(
        density_all.reshape(2 * pair_rows, -1),
        screen.reshape(2 * panel_rows, -1),
        (((1,), (1,)), ((), ())),
        preferred_element_type=jnp.float32,
    )
    product = product.reshape(2, pair_rows, 2, panel_rows)
    return (product[0, :, 0] - product[1, :, 1], product[0, :, 1] + product[1, :, 0])


def plain_body(densities, screened, energies, occupied, kmq, offsets, weights):
    qpoint = lax.axis_index("pb")
    my_freq = lax.axis_index("freq")
    my_panel = lax.axis_index("ga")
    count_pb = lax.axis_size("pb")
    count_freq = lax.axis_size("freq")
    screen = screened[0, 0]
    panel_width = screen.shape[1]
    local_block = densities[0]
    whole = lax.all_gather(local_block, ("freq", "ga"), axis=1, tiled=True)
    real_x, imag_x = panel_product(whole, screen)
    own_rows = lax.dynamic_slice_in_dim(whole, my_panel * panel_width, panel_width, 2)
    dense = own_rows.astype(jnp.float32)
    real_sum = jnp.sum(dense[0] * real_x + dense[1] * imag_x, axis=1)
    imag_sum = jnp.sum(dense[0] * imag_x - dense[1] * real_x, axis=1)
    pair_total = lax.psum(jnp.stack([real_sum, imag_sum]), "ga")
    weighted = (pair_total * weights[my_freq]).reshape(2, NS, NB)
    kpoint = kmq[qpoint]
    level_row = energies[kpoint]
    filled = occupied[kpoint]
    total_out = OUT_DEV * count_pb * count_freq
    index_grid = (jnp.arange(count_pb, dtype=jnp.int32)[:, None] * count_freq + my_freq) * OUT_DEV
    index_grid = (index_grid + jnp.arange(OUT_DEV, dtype=jnp.int32)[None, :]).reshape(-1)
    omegas = -2.0 + 4.0 * index_grid.astype(jnp.float32) / total_out
    summed = jnp.zeros((2, NS, count_pb * OUT_DEV), jnp.float32)
    passed = weighted
    for rotation in range(count_freq):
        anchor = (my_freq - rotation) % count_freq
        freq_shift = 4.0 * offsets[anchor].astype(jnp.float32) / total_out
        green_real, green_imag = green_parts(level_row, filled, freq_shift, omegas)
        summed = summed + spectrum(passed[0], passed[1], green_real, green_imag)
        if rotation + 1 < count_freq:
            passed = from_behind(passed, "freq", 1)
    local_part = lax.psum_scatter(summed, "pb", scatter_dimension=2, tiled=True)
    prefactor = 1.0 / (2.0 * math.pi * count_pb)
    return jnp.stack([-prefactor * local_part[1], prefactor * local_part[0]])


def fused_kernel(
    shape,
    dens_ref,
    screen_ref,
    energy_ref,
    filled_ref,
    kmq_ref,
    offset_ref,
    weight_ref,
    out_ref,
    blocks,
    panel,
    acc,
    green,
    parts,
    own_sem,
    panel_sem,
    send_sem,
    recv_sem,
    part_send,
    part_recv,
    ready,
):
    count_pb, count_freq, count_ga, chunks, width, tile = shape
    group = count_freq * count_ga
    pair_rows = blocks.shape[3]
    pairs = group * pair_rows
    panel_rows = panel.shape[2]
    total_out = green.shape[2]
    qpoint = lax.axis_index("pb")
    freq = lax.axis_index("freq")
    x = lax.axis_index("ga")
    y, core = freq // 2, freq % 2
    ny, nx, nc = 1 - y, 1 - x, 1 - core

    def place(yy, cc, xx):
        return (yy * 2 + cc) * count_ga + xx

    me = place(y, core, x)
    at_x = {"freq": freq, "ga": nx}
    at_y = {"freq": ny * 2 + core, "ga": x}
    at_core = {"freq": y * 2 + nc, "ga": x}
    onward = {"freq": (y + core * (1 - 2 * y)) * 2 + core, "ga": x + (1 - core) * (1 - 2 * x)}
    passed = place(y + (1 - core) * (1 - 2 * y), core, x + core * (1 - 2 * x))
    from_x = place(y, core, nx)
    from_y = place(ny, core, x)
    across = place(ny, core, nx)
    mine = (me, from_x, from_y, across)
    theirs = (place(y, nc, x), place(y, nc, nx), place(ny, nc, x), place(ny, nc, nx))

    def own_copy(k):
        return pltpu.make_async_copy(
            dens_ref.at[0, :, :, pl.ds(k * width, width)], blocks.at[k, me], own_sem.at[k]
        )

    def panel_copy(k):
        return pltpu.make_async_copy(
            screen_ref.at[0, 0, :, :, pl.ds(k * width, width)], panel.at[k], panel_sem.at[k]
        )

    def remote(k, lane, block, target):
        return pltpu.make_async_remote_copy(
            src_ref=blocks.at[k, block],
            dst_ref=blocks.at[k, block],
            send_sem=send_sem.at[lane, k],
            recv_sem=recv_sem.at[lane, k],
            device_id=target,
            device_id_type=MESH,
        )

    for k in range(chunks):
        own_copy(k).start()
    for k in range(chunks):
        panel_copy(k).start()

    barrier = pltpu.get_barrier_semaphore()
    peers = []
    for step in range(1, count_pb * group):
        layer = (qpoint + step // group) % count_pb
        spot = (me + step) % group
        peers.append({"pb": layer, "freq": spot // count_ga, "ga": spot % count_ga})
    layers = [{"pb": (qpoint + step) % count_pb} for step in range(1, count_pb)]
    near = [at_x, at_y, at_core] + layers
    for target in near:
        pl.semaphore_signal(barrier, inc=1, device_id=target, device_id_type=MESH)
    pl.semaphore_wait(barrier, len(near))

    def send_own(k):
        own_copy(k).wait()
        remote(k, 0, me, at_x).start()
        remote(k, 1, me, at_y).start()
        remote(k, 3, me, at_core).start()

    def pass_on(k):
        remote(k, 0, from_x, at_x).wait_recv()
        remote(k, 1, from_y, at_y).wait_recv()
        remote(k, 2, passed, onward).start()
        remote(k, 4, from_x, at_core).start()
        remote(k, 5, from_y, at_core).start()

    def share_across(k):
        remote(k, 2, across, onward).wait_recv()
        remote(k, 6, across, at_core).start()

    def arrive(k):
        for which in range(4):
            remote(k, 3 + which, theirs[which], at_core).wait_recv()
        panel_copy(k).wait()

    for k in range(AHEAD):
        send_own(k)

    kpoint = kmq_ref[qpoint]
    level_row = energy_ref[pl.ds(kpoint, 1), :]
    levels = jnp.broadcast_to(level_row, (8, level_row.shape[1])).T[:, :1]
    bands = lax.broadcasted_iota(jnp.int32, (level_row.shape[1], total_out), 0)
    grid = lax.broadcasted_iota(jnp.int32, (level_row.shape[1], total_out), 1)
    omegas = -2.0 + 4.0 * grid.astype(jnp.float32) / total_out
    freq_shift = 4.0 * offset_ref[freq].astype(jnp.float32) / total_out
    real_part = omegas - freq_shift - levels
    imag_part = jnp.where(bands < filled_ref[kpoint], -broadening, broadening)
    scale = weight_ref[freq] / (2.0 * math.pi * count_pb)
    inverse = scale / (real_part * real_part + imag_part * imag_part)
    green[0] = real_part * inverse
    green[1] = -imag_part * inverse

    tiles = panel_rows // tile
    pass_on(0)
    pass_on(1)
    share_across(0)
    for k in range(chunks):
        if k + AHEAD < chunks:
            send_own(k + AHEAD)
        if k + 2 < chunks:
            pass_on(k + 2)
        arrive(k)
        if k == chunks - 2:
            for target in layers:
                pl.semaphore_signal(ready, inc=1, device_id=target, device_id_type=MESH)
        for plane in range(2):
            if plane == 1:
                if k + 1 < chunks:
                    share_across(k + 1)

            @pl.loop(0, tiles)
            def _(t):
                rows = pl.ds(pl.multiple_of(t * tile, tile), tile)
                left = blocks[k].reshape(2 * pairs, width)
                value = lax.dot_general(
                    left,
                    panel[k, plane, rows, :],
                    (((1,), (1,)), ((), ())),
                    preferred_element_type=jnp.float32,
                )
                if k == 0:
                    acc[plane, :, rows] = value
                else:
                    acc[plane, :, rows] += value

    chunks_here = panel_rows // width
    spread = 128
    sums = []
    for b in range(group):
        def add_chunk(t, totals):
            real_total, imag_total = totals
            for part in range(width // spread):
                dense = blocks[x * chunks_here + t, b, :, :, part * spread : (part + 1) * spread]
                dense = dense.astype(jnp.float32)
                cols = pl.ds(pl.multiple_of(t * width, width) + part * spread, spread)
                low = pl.ds(2 * b * pair_rows, pair_rows)
                high = pl.ds((2 * b + 1) * pair_rows, pair_rows)
                real_x = acc[0, low, cols] - acc[1, high, cols]
                imag_x = acc[1, low, cols] + acc[0, high, cols]
                real_total = real_total + dense[0] * real_x + dense[1] * imag_x
                imag_total = imag_total + dense[0] * imag_x - dense[1] * real_x
            return real_total, imag_total

        zero = jnp.zeros((pair_rows, spread), jnp.float32)
        sums.append(lax.fori_loop(0, chunks_here, add_chunk, (zero, zero)))
    pair_real = jnp.sum(jnp.concatenate([s[0] for s in sums]), axis=1, keepdims=True)
    pair_imag = jnp.sum(jnp.concatenate([s[1] for s in sums]), axis=1, keepdims=True)
    real_out = jnp.sum(pair_real * green[0] - pair_imag * green[1], axis=0, keepdims=True)
    imag_out = jnp.sum(pair_real * green[1] + pair_imag * green[0], axis=0, keepdims=True)

    parts[0, 0:1] = -imag_out
    parts[0, 1:2] = real_out
    pl.semaphore_wait(ready, len(layers))
    copies = []
    for step, target in enumerate(peers, 1):
        copy = pltpu.make_async_remote_copy(
            src_ref=parts.at[0],
            dst_ref=parts.at[step],
            send_sem=part_send.at[step],
            recv_sem=part_recv.at[step],
            device_id=target,
            device_id_type=MESH,
        )
        copy.start()
        copies.append(copy)
    for copy in copies:
        copy.wait_recv()
    total = jnp.sum(parts[...], axis=0)
    first = (qpoint * count_freq + freq) * OUT_DEV
    lanes = lax.broadcasted_iota(jnp.int32, total.shape, 1)
    spots = lax.broadcasted_iota(jnp.int32, (2, OUT_DEV), 1)
    result = jnp.zeros((2, OUT_DEV), jnp.float32)
    for j in range(OUT_DEV):
        picked = jnp.sum(jnp.where(lanes == first + j, total, 0.0), axis=1, keepdims=True)
        result = jnp.where(spots == j, picked, result)
    out_ref[...] = result.reshape(out_ref.shape)

    for copy in copies:
        copy.wait_send()
    for k in range(chunks):
        remote(k, 0, me, at_x).wait_send()
        remote(k, 1, me, at_y).wait_send()
        remote(k, 2, passed, onward).wait_send()
        for which in range(4):
            remote(k, 3 + which, mine[which], at_core).wait_send()


def fused_body(densities, screened, energies, occupied, kmq, offsets, weights):
    count_pb = lax.axis_size("pb")
    count_freq = lax.axis_size("freq")
    count_ga = lax.axis_size("ga")
    pair_rows, basis = densities.shape[2:]
    panel_rows = screened.shape[3]
    group = count_freq * count_ga
    pairs = group * pair_rows
    width = basis // CHUNKS
    total_out = OUT_DEV * count_pb * count_freq
    shape = (count_pb, count_freq, count_ga, CHUNKS, width, min(TILE, panel_rows))
    anywhere = pl.BlockSpec(memory_space=pl.ANY)
    scalar = pl.BlockSpec(memory_space=pltpu.SMEM)
    vector = pl.BlockSpec(memory_space=pltpu.VMEM)
    return pl.pallas_call(
        functools.partial(fused_kernel, shape),
        out_shape=jax.ShapeDtypeStruct((2, NS, OUT_DEV), jnp.float32),
        in_specs=[anywhere, anywhere, vector, scalar, scalar, scalar, scalar],
        out_specs=vector,
        scratch_shapes=[
            pltpu.VMEM((CHUNKS, group, 2, pair_rows, width), jnp.bfloat16),
            pltpu.VMEM((CHUNKS, 2, panel_rows, width), jnp.bfloat16),
            pltpu.VMEM((2, 2 * pairs, panel_rows), jnp.float32),
            pltpu.VMEM((2, NB, total_out), jnp.float32),
            pltpu.VMEM((count_pb * group, 2, total_out), jnp.float32),
            pltpu.SemaphoreType.DMA((CHUNKS,)),
            pltpu.SemaphoreType.DMA((CHUNKS,)),
            pltpu.SemaphoreType.DMA((7, CHUNKS)),
            pltpu.SemaphoreType.DMA((7, CHUNKS)),
            pltpu.SemaphoreType.DMA((count_pb * group,)),
            pltpu.SemaphoreType.DMA((count_pb * group,)),
            pltpu.SemaphoreType.REGULAR,
        ],
        compiler_params=pltpu.CompilerParams(
            collective_id=0, has_side_effects=True, vmem_limit_bytes=58 * 2**20
        ),
    )(densities, screened, energies, occupied, kmq, offsets, weights)


def body(densities, screened, *rest):
    chips = lax.axis_size("freq") == 4 and lax.axis_size("ga") == 2
    if chips and densities.shape[2] % 16 == 0 and densities.shape[3] % (CHUNKS * 128) == 0:
        return fused_body(densities, screened, *rest)
    return plain_body(densities, screened, *rest)


def solution(mesh):
    placed = (
        P("pb", None, ("freq", "ga"), None),
        P("pb", "freq", None, "ga", None),
        P(),
        P(),
        P(),
        P(),
        P(),
    )
    return jax.shard_map(
        body, mesh=mesh, in_specs=placed, out_specs=P(None, None, ("pb", "freq")), check_vma=False
    )
```

profile of v0, /device:TPU:0, one launch (start us, length us, event | category | flops | bytes accessed | tf_op | source)
XLA Modules:
  0.0 46.0 jit_solution(13572493375992274805)
XLA Ops:
  0.0 44.8 %shard_map.73 = f32[2,1,4]{2,1,0:T(1,128)} custom-call(bf16[1,2,32,4096]{3,2,1,0:T(8,128)(2,1)} %dens_ref.1, bf16[1,1,2,2048,4096]{4,3,2,1,0:T(8,128)(2,1)} %screen_ref.1, f32[16,256]{1,0:T(8,128)} %energy_ref.1, s32[16]{0:T(128)} %filled_ref.1, s32[4]{0:T(128)} %kmq_ref.1, s32[4]{0:T(128)} %offset_ref.1, f32[4]{0:T(128)} %weight_ref.1), custom_call_target="tpu_custom_call" | custom-call | tf_op jit(solution)/shard_map/pallas_call | solution.py:336
  44.8 1.2 %copy.9 = f32[2,1,4]{2,1,0:T(1,128)} copy(f32[2,1,4]{2,1,0:T(1,128)} %shard_map.73) | data formatting | bytes 64
where the time goes:
time: 46.2 us; the launch traced here: 46 us
  Pallas kernels  44.8 us (97%)
  local copies, waits for them, and re-layouts  1.24 us (3%)
    pallas_call x1, Pallas kernels, fused_body(): pl.pallas_call(functools.partial(fused_kernel, shape), out_shape=jax.Shap...  44.8 us
    unnamed x1, local copies, waits for them, and re-layouts  1.24 us

commit v1 on v0

v1 whole, which is shorter than its diff:
```python
import functools
import math

import jax
import jax.numpy as jnp
from jax import lax
from jax.experimental import pallas as pl
from jax.experimental.pallas import tpu as pltpu
from jax.sharding import PartitionSpec as P

MESH = pl.DeviceIdType.MESH
CHUNKS = 4
PANELS = 8
HALF = CHUNKS // 2
SLOTS = 8

NB = 256
NS = 1
OUT_DEV = 4


broadening = 0.15


def from_behind(block, axis, distance):
    devices = range(lax.axis_size(axis))
    route = [((i - distance) % len(devices), i) for i in devices]
    return lax.ppermute(block, axis, route)


def green_parts(level_row, filled, freq_shift, omegas):
    bands = jnp.arange(level_row.shape[0], dtype=jnp.int32)
    pole_sign = jnp.where(bands < filled, -1.0, 1.0).astype(jnp.float32)
    real_part = omegas[None, :] - freq_shift - level_row[:, None]
    imag_part = broadening * pole_sign[:, None]
    denominator = real_part * real_part + imag_part * imag_part
    return (real_part / denominator, -imag_part / denominator)


def spectrum(pair_real, pair_imag, green_real, green_imag):
    exact = lax.Precision.HIGHEST
    real_out = jnp.dot(pair_real, green_real, precision=exact) - jnp.dot(
        pair_imag, green_imag, precision=exact
    )
    imag_out = jnp.dot(pair_real, green_imag, precision=exact) + jnp.dot(
        pair_imag, green_real, precision=exact
    )
    return jnp.stack([real_out, imag_out])


def panel_product(density_all, screen):
    pair_rows = density_all.shape[1]
    panel_rows = screen.shape[1]
    product = lax.dot_general(
        density_all.reshape(2 * pair_rows, -1),
        screen.reshape(2 * panel_rows, -1),
        (((1,), (1,)), ((), ())),
        preferred_element_type=jnp.float32,
    )
    product = product.reshape(2, pair_rows, 2, panel_rows)
    return (product[0, :, 0] - product[1, :, 1], product[0, :, 1] + product[1, :, 0])


def plain_body(densities, screened, energies, occupied, kmq, offsets, weights):
    qpoint = lax.axis_index("pb")
    my_freq = lax.axis_index("freq")
    my_panel = lax.axis_index("ga")
    count_pb = lax.axis_size("pb")
    count_freq = lax.axis_size("freq")
    screen = screened[0, 0]
    panel_width = screen.shape[1]
    local_block = densities[0]
    whole = lax.all_gather(local_block, ("freq", "ga"), axis=1, tiled=True)
    real_x, imag_x = panel_product(whole, screen)
    own_rows = lax.dynamic_slice_in_dim(whole, my_panel * panel_width, panel_width, 2)
    dense = own_rows.astype(jnp.float32)
    real_sum = jnp.sum(dense[0] * real_x + dense[1] * imag_x, axis=1)
    imag_sum = jnp.sum(dense[0] * imag_x - dense[1] * real_x, axis=1)
    pair_total = lax.psum(jnp.stack([real_sum, imag_sum]), "ga")
    weighted = (pair_total * weights[my_freq]).reshape(2, NS, NB)
    kpoint = kmq[qpoint]
    level_row = energies[kpoint]
    filled = occupied[kpoint]
    total_out = OUT_DEV * count_pb * count_freq
    index_grid = (jnp.arange(count_pb, dtype=jnp.int32)[:, None] * count_freq + my_freq) * OUT_DEV
    index_grid = (index_grid + jnp.arange(OUT_DEV, dtype=jnp.int32)[None, :]).reshape(-1)
    omegas = -2.0 + 4.0 * index_grid.astype(jnp.float32) / total_out
    summed = jnp.zeros((2, NS, count_pb * OUT_DEV), jnp.float32)
    passed = weighted
    for rotation in range(count_freq):
        anchor = (my_freq - rotation) % count_freq
        freq_shift = 4.0 * offsets[anchor].astype(jnp.float32) / total_out
        green_real, green_imag = green_parts(level_row, filled, freq_shift, omegas)
        summed = summed + spectrum(passed[0], passed[1], green_real, green_imag)
        if rotation + 1 < count_freq:
            passed = from_behind(passed, "freq", 1)
    local_part = lax.psum_scatter(summed, "pb", scatter_dimension=2, tiled=True)
    prefactor = 1.0 / (2.0 * math.pi * count_pb)
    return jnp.stack([-prefactor * local_part[1], prefactor * local_part[0]])


def fused_kernel(
    shape,
    dens_hbm,
    screen_hbm,
    energy_hbm,
    filled_hbm,
    kmq_hbm,
    offset_hbm,
    weight_hbm,
    out_ref,
    dens,
    minus,
    panel,
    acc,
    psum,
    green,
    parts,
    energy,
    filled,
    kmq,
    offset,
    weight,
    own_sem,
    panel_sem,
    small_sem,
    send_sem,
    recv_sem,
    part_send,
    part_recv,
    ready,
):
    count_pb, count_freq, count_ga = shape
    group = count_freq * count_ga
    rows = dens.shape[3]
    width = dens.shape[4]
    cols = panel.shape[3]
    per = width // cols
    total_out = green.shape[2]
    qpoint = lax.axis_index("pb")
    freq = lax.axis_index("freq")
    x = lax.axis_index("ga")
    y, core = freq // 2, freq % 2
    ny, nx, nc = 1 - y, 1 - x, 1 - core
    at_x = {"freq": freq, "ga": nx}
    at_y = {"freq": ny * 2 + core, "ga": x}
    at_core = {"freq": y * 2 + nc, "ga": x}

    def place(yy, cc, xx):
        return (yy * 2 + cc) * count_ga + xx

    def owner(slot):
        dy, dx, dc = slot // 4, slot // 2 % 2, slot % 2
        return place((y + dy) % 2, (core + dc) % 2, (x + dx) % 2)

    barrier = pltpu.get_barrier_semaphore()
    for target in (at_x, at_y, at_core):
        pl.semaphore_signal(barrier, inc=1, device_id=target, device_id_type=MESH)

    def both_layers(semaphore):
        @pl.when(qpoint > 0)
        def _():
            pl.semaphore_signal(
                semaphore, inc=1, device_id={"pb": qpoint - 1}, device_id_type=MESH
            )

        @pl.when(qpoint < count_pb - 1)
        def _():
            pl.semaphore_signal(
                semaphore, inc=1, device_id={"pb": qpoint + 1}, device_id_type=MESH
            )

    layers = (qpoint + count_pb - 1) // count_pb + (2 * count_pb - 2 - qpoint) // count_pb
    both_layers(barrier)

    def own_copy(r):
        start = pl.multiple_of((x * HALF + r) % CHUNKS * width, width)
        return pltpu.make_async_copy(
            dens_hbm.at[0, :, :, pl.ds(start, width)], dens.at[r, 0], own_sem.at[r]
        )

    def panel_copy(n):
        start = pl.multiple_of((x * (PANELS // 2) + n) % PANELS * cols, cols)
        return pltpu.make_async_copy(
            screen_hbm.at[0, 0, :, :, pl.ds(start, cols)], panel.at[n], panel_sem.at[n]
        )

    first_own = [HALF + r for r in range(HALF)] + list(range(HALF))
    for r in range(CHUNKS):
        own_copy(r).start()
    small = [
        pltpu.make_async_copy(source, target, small_sem.at[i])
        for i, (source, target) in enumerate(
            [
                (energy_hbm, energy),
                (filled_hbm, filled),
                (kmq_hbm, kmq),
                (offset_hbm, offset),
                (weight_hbm, weight),
            ]
        )
    ]
    for copy in small:
        copy.start()
    for n in range(PANELS):
        panel_copy(n).start(priority=1)

    def remote(lane, r, slot, there, slot_there, target):
        return pltpu.make_async_remote_copy(
            src_ref=dens.at[r, slot],
            dst_ref=dens.at[there, slot_there],
            send_sem=send_sem.at[lane, r],
            recv_sem=recv_sem.at[there, slot_there],
            device_id=target,
            device_id_type=MESH,
        )

    def to_x(r):
        return remote(0, r, 0, (r + HALF) % CHUNKS, 2, at_x)

    def to_y(r):
        return remote(1, r, 0, r, 4, at_y)

    def to_core(r):
        return remote(2, r, 0, r, 1, at_core)

    def onward_y(r):
        return remote(3, r, 2, r, 6, at_y)

    def relay_x(r):
        return pltpu.make_async_remote_copy(
            src_ref=dens.at[r, 4],
            dst_ref=dens.at[r + HALF, 6],
            send_sem=send_sem.at[3, r + HALF],
            recv_sem=recv_sem.at[r + HALF, 6],
            device_id=at_x,
            device_id_type=MESH,
        )

    def share(r, slot):
        return remote(3 + slot // 2, r, slot, r, slot + 1, at_core)

    def arrived(r, slot):
        remote(0, r, slot, r, slot, at_x).wait_recv()

    def take(r, slot):
        arrived(r, slot)
        share(r, slot).start()

    def pass_ready(step):
        if step < count_pb - 1:
            pl.semaphore_wait(ready.at[step - 1], layers)
            both_layers(ready.at[step])

    def prepare(r, slots):
        for slot in slots:
            minus[r, slot] = -dens[r, slot, 1]

    with jax.named_scope("bar"):
        pl.semaphore_wait(barrier, 3 + layers)
    for r in first_own:
        with jax.named_scope(f"own{r}"):
            own_copy(r).wait()
        if r >= HALF:
            to_x(r).start()
        else:
            to_y(r).start()
        to_core(r).start()
    for r in range(HALF):
        to_x(r).start()

    with jax.named_scope("small"):
        for copy in small:
            copy.wait()
    kpoint = kmq[qpoint]
    level_row = energy[pl.ds(kpoint, 1), :]
    levels = jnp.broadcast_to(level_row, (8, level_row.shape[1])).T[:, :1]
    bands = lax.broadcasted_iota(jnp.int32, (level_row.shape[1], total_out), 0)
    grid = lax.broadcasted_iota(jnp.int32, (level_row.shape[1], total_out), 1)
    omegas = -2.0 + 4.0 * grid.astype(jnp.float32) / total_out
    freq_shift = 4.0 * offset[freq].astype(jnp.float32) / total_out
    real_part = omegas - freq_shift - levels
    imag_part = jnp.where(bands < filled[kpoint], -broadening, broadening)
    scale = weight[freq] / (2.0 * math.pi * count_pb)
    inverse = scale / (real_part * real_part + imag_part * imag_part)
    green[0] = real_part * inverse
    green[1] = -imag_part * inverse

    def product(slots, chunks, n):
        low = chunks[0] * width
        depth = len(chunks) * width
        left = []
        for plane in range(2):
            for r in chunks:
                pieces = []
                for slot in slots:
                    if plane == 0:
                        pieces += [dens[r, slot, 0], minus[r, slot]]
                    else:
                        pieces += [dens[r, slot, 1], dens[r, slot, 0]]
                left.append(jnp.concatenate(pieces, axis=0))
        right = [panel[n, plane, low : low + depth, :] for plane in range(2)]
        return lax.dot_general(
            jnp.concatenate(left, axis=1),
            jnp.concatenate(right, axis=0),
            (((1,), (0,)), ((), ())),
            preferred_element_type=jnp.float32,
        )

    started = set()

    def reduce(value, slots, n):
        r, off = n // per, n % per * cols
        for i, slot in enumerate(slots):
            real_y = value[2 * i * rows : (2 * i + 1) * rows]
            imag_y = value[(2 * i + 1) * rows : (2 * i + 2) * rows]
            real_d = dens[r, slot, 0, :, off : off + cols].astype(jnp.float32)
            imag_d = dens[r, slot, 1, :, off : off + cols].astype(jnp.float32)
            real = real_y * real_d - imag_y * imag_d
            imag = real_y * imag_d + imag_y * real_d
            for c, total in enumerate((real, imag)):
                narrow = total[:, :128]
                for part in range(1, cols // 128):
                    narrow = narrow + total[:, part * 128 : (part + 1) * 128]
                if slot in started:
                    psum[c, slot] += narrow
                else:
                    psum[c, slot] = narrow
            started.add(slot)

    def spectra(slots):
        real_out = jnp.zeros((rows, total_out), jnp.float32)
        imag_out = jnp.zeros((rows, total_out), jnp.float32)
        for slot in slots:
            pair_real = jnp.sum(psum[0, slot], axis=1, keepdims=True)
            pair_imag = jnp.sum(psum[1, slot], axis=1, keepdims=True)
            here = pl.ds(pl.multiple_of(owner(slot) * rows, rows), rows)
            green_real, green_imag = green[0, here, :], green[1, here, :]
            real_out = real_out + pair_real * green_real - pair_imag * green_imag
            imag_out = imag_out + pair_real * green_imag + pair_imag * green_real
        return real_out, imag_out

    head = list(range(HALF))
    near, far = (2, 3, 4, 5), (6, 7)

    def own_block(n):
        with jax.named_scope(f"pan{n}"):
            panel_copy(n).wait()
        reduce(product((0, 1), head, n), (0, 1), n)

    def near_first(n):
        acc[n] = product(near, [0], n)

    def near_last(n):
        value = acc[n] + product(near, [1], n)
        if n < PANELS // 2:
            reduce(value, near, n)
        else:
            reduce(value[: 4 * rows], near[:2], n)
            acc[n, 4 * rows :, :] = value[4 * rows :]

    def far_block(n):
        value = product(far, head, n)
        reduce(value, far, n)
        if n >= PANELS // 2:
            reduce(acc[n, 4 * rows :, :], near[2:], n)

    for r in head:
        prepare(r, (0,))
    with jax.named_scope("sib"):
        for r in range(CHUNKS):
            arrived(r, 1)
    for r in head:
        prepare(r, (1,))
    for n in range(4):
        own_block(n)
    with jax.named_scope("take0"):
        take(0, 2)
        onward_y(0).start()
        take(0, 4)
        relay_x(0).start()
    own_block(4)
    with jax.named_scope("got0"):
        arrived(0, 3)
        arrived(0, 5)
    prepare(0, near)
    near_first(0)
    with jax.named_scope("take1"):
        take(1, 2)
        onward_y(1).start()
        for r in range(HALF, CHUNKS):
            to_y(r).start()
        take(1, 4)
        relay_x(1).start()
    own_block(5)
    near_first(1)
    own_block(6)
    near_first(2)
    own_block(7)
    near_first(3)
    with jax.named_scope("take2"):
        take(2, 2)
        take(0, 6)
    for n in range(4, PANELS):
        near_first(n)
    with jax.named_scope("take3"):
        arrived(1, 3)
        arrived(1, 5)
        take(3, 2)
        take(1, 6)
        arrived(0, 7)
        both_layers(ready.at[0])
    prepare(1, near)
    for n in range(4):
        near_last(n)
    with jax.named_scope("take4"):
        arrived(2, 3)
        arrived(3, 3)
        take(2, 4)
        take(2, 6)
        pass_ready(1)
    for n in range(4, PANELS):
        near_last(n)
    with jax.named_scope("take5"):
        arrived(1, 7)
        take(3, 4)
        take(3, 6)
        for step in range(2, count_pb - 1):
            pass_ready(step)
    early = spectra((0, 1, 2, 3))
    for r in head:
        prepare(r, far)
    for n in range(4):
        far_block(n)
    with jax.named_scope("last"):
        for r in range(HALF, CHUNKS):
            arrived(r, 5)
            arrived(r, 7)
    for n in range(4, PANELS):
        far_block(n)
    final = spectra((4, 5, 6, 7))
    parts[0, 0:1] = -jnp.sum(early[1] + final[1], axis=0, keepdims=True)
    parts[0, 1:2] = jnp.sum(early[0] + final[0], axis=0, keepdims=True)
    with jax.named_scope("ready"):
        pl.semaphore_wait(ready.at[count_pb - 2], layers)
    me = owner(0)
    copies = []
    for step in range(1, count_pb * group):
        spot = (me + step) % group
        target = {
            "pb": (qpoint + step // group) % count_pb,
            "freq": spot // count_ga,
            "ga": spot % count_ga,
        }
        copy = pltpu.make_async_remote_copy(
            src_ref=parts.at[0],
            dst_ref=parts.at[step],
            send_sem=part_send.at[step],
            recv_sem=part_recv.at[step],
            device_id=target,
            device_id_type=MESH,
        )
        copy.start()
        copies.append(copy)
    with jax.named_scope("drain"):
        for r in range(CHUNKS):
            to_x(r).wait_send()
            to_y(r).wait_send()
            to_core(r).wait_send()
            for slot in (2, 4, 6):
                share(r, slot).wait_send()
        for r in head:
            onward_y(r).wait_send()
            relay_x(r).wait_send()
    with jax.named_scope("exch"):
        for copy in copies:
            copy.wait_recv()
    total = jnp.sum(parts[...], axis=0)
    first = (qpoint * count_freq + freq) * OUT_DEV
    lanes = lax.broadcasted_iota(jnp.int32, total.shape, 1)
    spots = lax.broadcasted_iota(jnp.int32, (2, OUT_DEV), 1)
    result = jnp.zeros((2, OUT_DEV), jnp.float32)
    for j in range(OUT_DEV):
        picked = jnp.sum(jnp.where(lanes == first + j, total, 0.0), axis=1, keepdims=True)
        result = jnp.where(spots == j, picked, result)
    out_ref[...] = result.reshape(out_ref.shape)
    with jax.named_scope("sent"):
        for copy in copies:
            copy.wait_send()


def fused_body(densities, screened, energies, occupied, kmq, offsets, weights):
    count_pb = lax.axis_size("pb")
    count_freq = lax.axis_size("freq")
    count_ga = lax.axis_size("ga")
    pair_rows, basis = densities.shape[2:]
    panel_rows = screened.shape[3]
    group = count_freq * count_ga
    width = basis // CHUNKS
    cols = basis // PANELS
    total_out = OUT_DEV * count_pb * count_freq
    shape = (count_pb, count_freq, count_ga)
    anywhere = pl.BlockSpec(memory_space=pltpu.HBM)
    vector = pl.BlockSpec(memory_space=pltpu.VMEM)
    return pl.pallas_call(
        functools.partial(fused_kernel, shape),
        out_shape=jax.ShapeDtypeStruct((2, NS, OUT_DEV), jnp.float32),
        in_specs=[anywhere] * 7,
        out_specs=vector,
        scratch_shapes=[
            pltpu.VMEM((CHUNKS, SLOTS, 2, pair_rows, width), jnp.bfloat16),
            pltpu.VMEM((HALF, SLOTS, pair_rows, width), jnp.bfloat16),
            pltpu.VMEM((PANELS, 2, panel_rows, cols), jnp.bfloat16),
            pltpu.VMEM((PANELS, 8 * pair_rows, cols), jnp.float32),
            pltpu.VMEM((2, SLOTS, pair_rows, 128), jnp.float32),
            pltpu.VMEM((2, NB, total_out), jnp.float32),
            pltpu.VMEM((count_pb * group, 2, total_out), jnp.float32),
            pltpu.VMEM(energies.shape, energies.dtype),
            pltpu.SMEM(occupied.shape, occupied.dtype),
            pltpu.SMEM(kmq.shape, kmq.dtype),
            pltpu.SMEM(offsets.shape, offsets.dtype),
            pltpu.SMEM(weights.shape, weights.dtype),
            pltpu.SemaphoreType.DMA((CHUNKS,)),
            pltpu.SemaphoreType.DMA((PANELS,)),
            pltpu.SemaphoreType.DMA((5,)),
            pltpu.SemaphoreType.DMA((7, CHUNKS)),
            pltpu.SemaphoreType.DMA((CHUNKS, SLOTS)),
            pltpu.SemaphoreType.DMA((count_pb * group,)),
            pltpu.SemaphoreType.DMA((count_pb * group,)),
            pltpu.SemaphoreType.REGULAR((count_pb - 1,)),
        ],
        compiler_params=pltpu.CompilerParams(
            collective_id=0, has_side_effects=True, vmem_limit_bytes=46 * 2**20
        ),
    )(
        *(
            pltpu.with_memory_space_constraint(operand, pltpu.HBM)
            for operand in (densities, screened, energies, occupied, kmq, offsets, weights)
        )
    )


def body(densities, screened, *rest):
    basis, panel_rows = densities.shape[3], screened.shape[3]
    chips = lax.axis_size("freq") == 4 and lax.axis_size("ga") == 2 and lax.axis_size("pb") > 1
    fits = densities.shape[2] % 16 == 0 and basis % (PANELS * 128) == 0 and panel_rows * 2 == basis
    if chips and fits:
        return fused_body(densities, screened, *rest)
    return plain_body(densities, screened, *rest)


def solution(mesh):
    placed = (
        P("pb", None, ("freq", "ga"), None),
        P("pb", "freq", None, "ga", None),
        P(),
        P(),
        P(),
        P(),
        P(),
    )
    return jax.shard_map(
        body, mesh=mesh, in_specs=placed, out_specs=P(None, None, ("pb", "freq")), check_vma=False
    )
```

time: 46.2 us -> 36.3 us (0.79)
  Pallas kernels: 44.8 us -> 35.6 us
  local copies, waits for them, and re-layouts: 1.24 us -> 0.56 us
    pallas_call x1, Pallas kernels: 44.8 us -> 35.6 us  [fused_body(): pl.pallas_call(functools.partial(fused_kernel, shape), out_shape=jax.Shap...]
    unnamed x1, local copies, waits for them, and re-layouts: 1.24 us -> 0.56 us
where the time goes in v1:
time: 36.3 us; the launch traced here: 36.2 us
  Pallas kernels  35.6 us (98%)
  local copies, waits for them, and re-layouts  0.56 us (2%)
    pallas_call x1, Pallas kernels, fused_body(): pl.pallas_call(functools.partial(fused_kernel, shape), out_shape=jax.Shap...  35.6 us

profile of v1, /device:TPU:0, one launch (start us, length us, event | category | flops | bytes accessed | tf_op | source)
XLA Modules:
  0.0 36.2 jit_solution(8254157479520021898)
XLA Ops:
  0.0 35.6 %shard_map.73 = f32[2,1,4]{2,1,0:T(1,128)S(1)} custom-call(bf16[1,2,32,4096]{3,2,1,0:T(8,128)(2,1)} %dens_hbm.1, bf16[1,1,2,2048,4096]{4,3,2,1,0:T(8,128)(2,1)} %screen_hbm.1, f32[16,256]{1,0:T(8,128)} %energy_hbm.1, s32[16]{0:T(128)} %filled_hbm.1, s32[4]{0:T(128)} %kmq_hbm.1, s32[4]{0:T(128)} %offset_hbm.1, f32[4]{0:T(128)} %weight_hbm.1), custom_call_target="tpu_custom_call" | custom-call | tf_op jit(solution)/shard_map/pallas_call | solution.py:505
  35.6 0.6 %copy.9 = f32[2,1,4]{2,1,0:T(1,128)} copy(f32[2,1,4]{2,1,0:T(1,128)S(1)} %shard_map.73) | data formatting | bytes 64

commit v2 on v1

--- a/solution.py
+++ b/solution.py
@@ -126,6 +126,7 @@
     small_sem,
     send_sem,
     recv_sem,
+    core_sem,
     part_send,
     part_recv,
     ready,
@@ -176,7 +177,7 @@
     def own_copy(r):
         start = pl.multiple_of((x * HALF + r) % CHUNKS * width, width)
         return pltpu.make_async_copy(
-            dens_hbm.at[0, :, :, pl.ds(start, width)], dens.at[r, 0], own_sem.at[r]
+            dens_hbm.at[0, :, :, pl.ds(start, width)], dens.at[r, 0], own_sem
         )
 
     def panel_copy(n):
@@ -205,47 +206,82 @@
     for n in range(PANELS):
         panel_copy(n).start(priority=1)
 
-    def remote(lane, r, slot, there, slot_there, target):
+    pairs = [((0, 2), (0, 4)), ((0, 3), (0, 5)), ((1, 2), (1, 4)), ((1, 3), (1, 5))]
+    pairs += [((2, 2), (0, 6)), ((3, 2), (1, 6)), ((2, 3), (3, 3)), ((2, 4), (2, 6))]
+    pairs += [((3, 4), (3, 6)), ((2, 5), (2, 7)), ((3, 5), (3, 7)), ((0, 7),), ((1, 7),)]
+    numbers = {block: i for i, pair in enumerate(pairs) for block in pair}
+
+    def remote(r, slot, there, slot_there, target, group_of):
         return pltpu.make_async_remote_copy(
             src_ref=dens.at[r, slot],
             dst_ref=dens.at[there, slot_there],
-            send_sem=send_sem.at[lane, r],
-            recv_sem=recv_sem.at[there, slot_there],
+            send_sem=send_sem.at[group_of],
+            recv_sem=recv_sem.at[numbers[there, slot_there]],
             device_id=target,
             device_id_type=MESH,
         )
 
     def to_x(r):
-        return remote(0, r, 0, (r + HALF) % CHUNKS, 2, at_x)
+        return remote(r, 0, (r + HALF) % CHUNKS, 2, at_x, r)
 
     def to_y(r):
-        return remote(1, r, 0, r, 4, at_y)
+        return remote(r, 0, r, 4, at_y, r)
 
     def to_core(r):
-        return remote(2, r, 0, r, 1, at_core)
+        return pltpu.make_async_remote_copy(
+            src_ref=dens.at[r, 0],
+            dst_ref=dens.at[r, 1],
+            send_sem=send_sem.at[r],
+            recv_sem=core_sem,
+            device_id=at_core,
+            device_id_type=MESH,
+        )
+
+    def siblings():
+        return pltpu.make_async_remote_copy(
+            src_ref=dens.at[:, 1],
+            dst_ref=dens.at[:, 1],
+            send_sem=send_sem.at[0],
+            recv_sem=core_sem,
+            device_id=at_core,
+            device_id_type=MESH,
+        )
 
     def onward_y(r):
-        return remote(3, r, 2, r, 6, at_y)
+        return remote(r, 2, r, 6, at_y, r)
 
     def relay_x(r):
-        return pltpu.make_async_remote_copy(
-            src_ref=dens.at[r, 4],
-            dst_ref=dens.at[r + HALF, 6],
-            send_sem=send_sem.at[3, r + HALF],
-            recv_sem=recv_sem.at[r + HALF, 6],
-            device_id=at_x,
+        return remote(r, 4, r + HALF, 6, at_x, r + HALF)
+
+    def share(r, slot):
+        return remote(r, slot, r, slot + 1, at_core, r)
+
+    def all_sent(r):
+        pltpu.make_async_remote_copy(
+            src_ref=dens.at[r, 1:],
+            dst_ref=dens.at[r, 1:],
+            send_sem=send_sem.at[r],
+            recv_sem=core_sem,
+            device_id=at_core,
             device_id_type=MESH,
-        )
-
-    def share(r, slot):
-        return remote(3 + slot // 2, r, slot, r, slot + 1, at_core)
-
-    def arrived(r, slot):
-        remote(0, r, slot, r, slot, at_x).wait_recv()
-
-    def take(r, slot):
-        arrived(r, slot)
-        share(r, slot).start()
+        ).wait_send()
+
+    def arrived(*blocks):
+        number = pairs.index(blocks)
+        landed = dens.at[0, 1 : 1 + len(blocks)]
+        pltpu.make_async_remote_copy(
+            src_ref=landed,
+            dst_ref=landed,
+            send_sem=send_sem.at[0],
+            recv_sem=recv_sem.at[number],
+            device_id=at_core,
+            device_id_type=MESH,
+        ).wait_recv()
+
+    def take(*blocks):
+        arrived(*blocks)
+        for r, slot in blocks:
+            share(r, slot).start()
 
     def pass_ready(step):
         if step < count_pb - 1:
@@ -258,9 +294,9 @@
 
     with jax.named_scope("bar"):
         pl.semaphore_wait(barrier, 3 + layers)
+    with jax.named_scope("own"):
+        pltpu.make_async_copy(dens.at[:, 0], dens.at[:, 0], own_sem).wait()
     for r in first_own:
-        with jax.named_scope(f"own{r}"):
-            own_copy(r).wait()
         if r >= HALF:
             to_x(r).start()
         else:
@@ -309,11 +345,36 @@
 
     started = set()
 
-    def reduce(value, slots, n):
+    def spectra(slots):
+        real_out = jnp.zeros((rows, total_out), jnp.float32)
+        imag_out = jnp.zeros((rows, total_out), jnp.float32)
+        for slot in slots:
+            pair_real = jnp.sum(psum[0, slot], axis=1, keepdims=True)
+            pair_imag = jnp.sum(psum[1, slot], axis=1, keepdims=True)
+            here = pl.ds(pl.multiple_of(owner(slot) * rows, rows), rows)
+            green_real, green_imag = green[0, here, :], green[1, here, :]
+            real_out = real_out + pair_real * green_real - pair_imag * green_imag
+            imag_out = imag_out + pair_real * green_imag + pair_imag * green_real
+        return real_out, imag_out
+
+    head = list(range(HALF))
+    half = PANELS // 2
+
+    def parts_of(value, slots):
+        return [(slot, value[2 * i * rows : 2 * (i + 1) * rows]) for i, slot in enumerate(slots)]
+
+    def first_part(slots, n):
+        for slot, value in parts_of(product(slots, [0], n), slots):
+            acc[n, slot] = value
+
+    def last_part(slots, n):
+        for slot, value in parts_of(product(slots, [1], n), slots):
+            acc[n, slot] += value
+
+    def settle(slots, n):
         r, off = n // per, n % per * cols
-        for i, slot in enumerate(slots):
-            real_y = value[2 * i * rows : (2 * i + 1) * rows]
-            imag_y = value[(2 * i + 1) * rows : (2 * i + 2) * rows]
+        for slot in slots:
+            real_y, imag_y = acc[n, slot, :rows], acc[n, slot, rows:]
             real_d = dens[r, slot, 0, :, off : off + cols].astype(jnp.float32)
             imag_d = dens[r, slot, 1, :, off : off + cols].astype(jnp.float32)
             real = real_y * real_d - imag_y * imag_d
@@ -328,153 +389,145 @@
                     psum[c, slot] = narrow
             started.add(slot)
 
-    def spectra(slots):
-        real_out = jnp.zeros((rows, total_out), jnp.float32)
-        imag_out = jnp.zeros((rows, total_out), jnp.float32)
-        for slot in slots:
-            pair_real = jnp.sum(psum[0, slot], axis=1, keepdims=True)
-            pair_imag = jnp.sum(psum[1, slot], axis=1, keepdims=True)
-            here = pl.ds(pl.multiple_of(owner(slot) * rows, rows), rows)
-            green_real, green_imag = green[0, here, :], green[1, here, :]
-            real_out = real_out + pair_real * green_real - pair_imag * green_imag
-            imag_out = imag_out + pair_real * green_imag + pair_imag * green_real
-        return real_out, imag_out
-
-    head = list(range(HALF))
-    near, far = (2, 3, 4, 5), (6, 7)
-
     def own_block(n):
         with jax.named_scope(f"pan{n}"):
             panel_copy(n).wait()
-        reduce(product((0, 1), head, n), (0, 1), n)
-
-    def near_first(n):
-        acc[n] = product(near, [0], n)
-
-    def near_last(n):
-        value = acc[n] + product(near, [1], n)
-        if n < PANELS // 2:
-            reduce(value, near, n)
-        else:
-            reduce(value[: 4 * rows], near[:2], n)
-            acc[n, 4 * rows :, :] = value[4 * rows :]
-
-    def far_block(n):
-        value = product(far, head, n)
-        reduce(value, far, n)
-        if n >= PANELS // 2:
-            reduce(acc[n, 4 * rows :, :], near[2:], n)
-
+        for slot, value in parts_of(product(own, head, n), own):
+            acc[n, slot] = value
+
+    own, xs, ys, far = (0, 1), (2, 3), (4, 5), (6, 7)
+    near, direct, shared = xs + ys, (2, 4), (3, 5)
     for r in head:
         prepare(r, (0,))
     with jax.named_scope("sib"):
-        for r in range(CHUNKS):
-            arrived(r, 1)
+        siblings().wait_recv()
     for r in head:
         prepare(r, (1,))
-    for n in range(4):
+    def finish(products, settled):
+        done = 0
+        for i, (slots, n) in enumerate(products):
+            last_part(slots, n)
+            until = len(settled) * (i + 1) // len(products)
+            for pair, m in settled[done:until]:
+                settle(pair, m)
+            done = until
+
+    own_block(0)
+    for n in range(1, half):
         own_block(n)
+        settle(own, n - 1)
     with jax.named_scope("take0"):
-        take(0, 2)
+        take((0, 2), (0, 4))
         onward_y(0).start()
-        take(0, 4)
         relay_x(0).start()
+    prepare(0, direct)
+    for n in range(3):
+        first_part(direct, n)
+    settle(own, 3)
     own_block(4)
     with jax.named_scope("got0"):
-        arrived(0, 3)
-        arrived(0, 5)
-    prepare(0, near)
-    near_first(0)
+        arrived((0, 3), (0, 5))
+    prepare(0, shared)
+    first_part(shared, 0)
+    settle(own, 4)
+    first_part(shared, 1)
+    first_part(shared, 2)
+    first_part(near, 3)
     with jax.named_scope("take1"):
-        take(1, 2)
+        take((1, 2), (1, 4))
         onward_y(1).start()
+        relay_x(1).start()
         for r in range(HALF, CHUNKS):
             to_y(r).start()
-        take(1, 4)
-        relay_x(1).start()
-    own_block(5)
-    near_first(1)
-    own_block(6)
-    near_first(2)
-    own_block(7)
-    near_first(3)
+        panel_copy(5).wait()
+        panel_copy(6).wait()
+    first_part(near, 4)
+    first_part(own + near, 5)
+    first_part(own + near, 6)
+    prepare(1, direct)
+    last_part(direct, 0)
+    last_part(direct, 1)
     with jax.named_scope("take2"):
-        take(2, 2)
-        take(0, 6)
-    for n in range(4, PANELS):
-        near_first(n)
+        take((2, 2), (0, 6))
+        arrived((1, 3), (1, 5))
+        panel_copy(7).wait()
+    first_part(own + near, 7)
+    prepare(1, shared)
+    last_part(shared, 0)
+    last_part(shared, 1)
+    steps = [(pair, n) for n in range(5) for pair in (xs, ys)]
+    finish(steps[4:], steps[:8])
     with jax.named_scope("take3"):
-        arrived(1, 3)
-        arrived(1, 5)
-        take(3, 2)
-        take(1, 6)
-        arrived(0, 7)
+        take((3, 2), (1, 6))
+        arrived((0, 7),)
         both_layers(ready.at[0])
-    prepare(1, near)
-    for n in range(4):
-        near_last(n)
+    prepare(0, far)
+    for n in range(PANELS):
+        first_part(far, n)
     with jax.named_scope("take4"):
-        arrived(2, 3)
-        arrived(3, 3)
-        take(2, 4)
-        take(2, 6)
+        take((2, 4), (2, 6))
+        arrived((1, 7),)
+        arrived((2, 3), (3, 3))
+    prepare(1, far)
+    steps = [(far, n) for n in range(PANELS)]
+    finish(steps[:1], [])
+    finish(steps[1:], [(xs, 4)] + steps[:4])
+    with jax.named_scope("take5"):
+        arrived((2, 5), (2, 7))
+        take((3, 4), (3, 6))
         pass_ready(1)
-    for n in range(4, PANELS):
-        near_last(n)
-    with jax.named_scope("take5"):
-        arrived(1, 7)
-        take(3, 4)
-        take(3, 6)
+    steps = [(pair, n) for n in (5, 6) for pair in (own, xs, ys)]
+    finish(steps[:1], [(ys, 4)])
+    finish(steps[1:], [(far, 4), steps[0], (far, 5), steps[1], steps[2], steps[3]])
+    with jax.named_scope("last3"):
+        arrived((3, 5), (3, 7))
         for step in range(2, count_pb - 1):
             pass_ready(step)
-    early = spectra((0, 1, 2, 3))
-    for r in head:
-        prepare(r, far)
-    for n in range(4):
-        far_block(n)
-    with jax.named_scope("last"):
-        for r in range(HALF, CHUNKS):
-            arrived(r, 5)
-            arrived(r, 7)
-    for n in range(4, PANELS):
-        far_block(n)
-    final = spectra((4, 5, 6, 7))
-    parts[0, 0:1] = -jnp.sum(early[1] + final[1], axis=0, keepdims=True)
-    parts[0, 1:2] = jnp.sum(early[0] + final[0], axis=0, keepdims=True)
+    finish([(own, 7), (xs, 7)], [(xs, 6), (ys, 6), (own, 7), (far, 6)])
+    finish([(ys, 7)], [(far, 7), (xs, 7)])
+    early = spectra((0, 1, 2, 3, 6, 7))
+    settle(ys, 7)
+    late = spectra((4, 5))
+    parts[0, 0:1] = -jnp.sum(early[1] + late[1], axis=0, keepdims=True)
+    parts[0, 1:2] = jnp.sum(early[0] + late[0], axis=0, keepdims=True)
     with jax.named_scope("ready"):
         pl.semaphore_wait(ready.at[count_pb - 2], layers)
     me = owner(0)
-    copies = []
-    for step in range(1, count_pb * group):
-        spot = (me + step) % group
-        target = {
-            "pb": (qpoint + step // group) % count_pb,
-            "freq": spot // count_ga,
-            "ga": spot % count_ga,
-        }
-        copy = pltpu.make_async_remote_copy(
-            src_ref=parts.at[0],
-            dst_ref=parts.at[step],
-            send_sem=part_send.at[step],
-            recv_sem=part_recv.at[step],
-            device_id=target,
-            device_id_type=MESH,
-        )
-        copy.start()
-        copies.append(copy)
+    down = qpoint < count_pb // 2
+    for turn in range(count_pb):
+        if turn < count_pb - 1:
+            high, low = count_pb - 1 - turn, turn
+            high = jnp.where(high > qpoint, high, high - 1)
+            low = jnp.where(low < qpoint, low, low + 1)
+            layer = jnp.where(down, high, low)
+        else:
+            layer = qpoint
+        turned = (layer + count_pb - qpoint) % count_pb * group
+        for step in range(group - 1, -1, -1):
+            if turn == count_pb - 1 and step == 0:
+                continue
+            spot = (me + step) % group
+            pltpu.make_async_remote_copy(
+                src_ref=parts.at[0],
+                dst_ref=parts.at[turned + step],
+                send_sem=part_send,
+                recv_sem=part_recv,
+                device_id={"pb": layer, "freq": spot // count_ga, "ga": spot % count_ga},
+                device_id_type=MESH,
+            ).start()
     with jax.named_scope("drain"):
         for r in range(CHUNKS):
-            to_x(r).wait_send()
-            to_y(r).wait_send()
-            to_core(r).wait_send()
-            for slot in (2, 4, 6):
-                share(r, slot).wait_send()
-        for r in head:
-            onward_y(r).wait_send()
-            relay_x(r).wait_send()
+            all_sent(r)
+    others = pltpu.make_async_remote_copy(
+        src_ref=parts.at[1:],
+        dst_ref=parts.at[1:],
+        send_sem=part_send,
+        recv_sem=part_recv,
+        device_id=at_core,
+        device_id_type=MESH,
+    )
     with jax.named_scope("exch"):
-        for copy in copies:
-            copy.wait_recv()
+        others.wait_recv()
     total = jnp.sum(parts[...], axis=0)
     first = (qpoint * count_freq + freq) * OUT_DEV
     lanes = lax.broadcasted_iota(jnp.int32, total.shape, 1)
@@ -485,8 +538,7 @@
         result = jnp.where(spots == j, picked, result)
     out_ref[...] = result.reshape(out_ref.shape)
     with jax.named_scope("sent"):
-        for copy in copies:
-            copy.wait_send()
+        others.wait_send()
 
 
 def fused_body(densities, screened, energies, occupied, kmq, offsets, weights):
@@ -511,7 +563,7 @@
             pltpu.VMEM((CHUNKS, SLOTS, 2, pair_rows, width), jnp.bfloat16),
             pltpu.VMEM((HALF, SLOTS, pair_rows, width), jnp.bfloat16),
             pltpu.VMEM((PANELS, 2, panel_rows, cols), jnp.bfloat16),
-            pltpu.VMEM((PANELS, 8 * pair_rows, cols), jnp.float32),
+            pltpu.VMEM((PANELS, SLOTS, 2 * pair_rows, cols), jnp.float32),
             pltpu.VMEM((2, SLOTS, pair_rows, 128), jnp.float32),
             pltpu.VMEM((2, NB, total_out), jnp.float32),
             pltpu.VMEM((count_pb * group, 2, total_out), jnp.float32),
@@ -520,17 +572,18 @@
             pltpu.SMEM(kmq.shape, kmq.dtype),
             pltpu.SMEM(offsets.shape, offsets.dtype),
             pltpu.SMEM(weights.shape, weights.dtype),
-            pltpu.SemaphoreType.DMA((CHUNKS,)),
+            pltpu.SemaphoreType.DMA,
             pltpu.SemaphoreType.DMA((PANELS,)),
             pltpu.SemaphoreType.DMA((5,)),
-            pltpu.SemaphoreType.DMA((7, CHUNKS)),
-            pltpu.SemaphoreType.DMA((CHUNKS, SLOTS)),
-            pltpu.SemaphoreType.DMA((count_pb * group,)),
-            pltpu.SemaphoreType.DMA((count_pb * group,)),
+            pltpu.SemaphoreType.DMA((CHUNKS,)),
+            pltpu.SemaphoreType.DMA((13,)),
+            pltpu.SemaphoreType.DMA,
+            pltpu.SemaphoreType.DMA,
+            pltpu.SemaphoreType.DMA,
             pltpu.SemaphoreType.REGULAR((count_pb - 1,)),
         ],
         compiler_params=pltpu.CompilerParams(
-            collective_id=0, has_side_effects=True, vmem_limit_bytes=46 * 2**20
+            collective_id=0, has_side_effects=True, vmem_limit_bytes=50 * 2**20
         ),
     )(
         *(

time: 36.3 us -> 34.2 us (0.942)
  Pallas kernels: 35.6 us -> 33.5 us
    pallas_call x1, Pallas kernels: 35.6 us -> 33.5 us  [fused_body(): pl.pallas_call(functools.partial(fused_kernel, shape), out_shape=jax.Shap...]
where the time goes in v2:
time: 34.2 us; the launch traced here: 34.1 us
  Pallas kernels  33.5 us (98%)
  local copies, waits for them, and re-layouts  0.56 us (2%)
    pallas_call x1, Pallas kernels, fused_body(): pl.pallas_call(functools.partial(fused_kernel, shape), out_shape=jax.Shap...  33.5 us

profile of v2, /device:TPU:0, one launch (start us, length us, event | category | flops | bytes accessed | tf_op | source)
XLA Modules:
  0.0 34.1 jit_solution(14635410500171948238)
XLA Ops:
  0.0 33.5 %shard_map.73 = f32[2,1,4]{2,1,0:T(1,128)S(1)} custom-call(bf16[1,2,32,4096]{3,2,1,0:T(8,128)(2,1)} %dens_hbm.1, bf16[1,1,2,2048,4096]{4,3,2,1,0:T(8,128)(2,1)} %screen_hbm.1, f32[16,256]{1,0:T(8,128)} %energy_hbm.1, s32[16]{0:T(128)} %filled_hbm.1, s32[4]{0:T(128)} %kmq_hbm.1, s32[4]{0:T(128)} %offset_hbm.1, f32[4]{0:T(128)} %weight_hbm.1), custom_call_target="tpu_custom_call" | custom-call | tf_op jit(solution)/shard_map/pallas_call | solution.py:557
  33.5 0.6 %copy.9 = f32[2,1,4]{2,1,0:T(1,128)} copy(f32[2,1,4]{2,1,0:T(1,128)S(1)} %shard_map.73) | data formatting | bytes 64

commit v3 on v2

--- a/solution.py
+++ b/solution.py
@@ -186,7 +186,6 @@
             screen_hbm.at[0, 0, :, :, pl.ds(start, cols)], panel.at[n], panel_sem.at[n]
         )
 
-    first_own = [HALF + r for r in range(HALF)] + list(range(HALF))
     for r in range(CHUNKS):
         own_copy(r).start()
     small = [
@@ -211,21 +210,26 @@
     pairs += [((3, 4), (3, 6)), ((2, 5), (2, 7)), ((3, 5), (3, 7)), ((0, 7),), ((1, 7),)]
     numbers = {block: i for i, pair in enumerate(pairs) for block in pair}
 
-    def remote(r, slot, there, slot_there, target, group_of):
+    cuts = [slice(0, width // 2), slice(width // 2, width)]
+
+    def remote(r, slot, there, slot_there, target, group_of, cut=slice(None)):
+        number = numbers[there, slot_there]
+        if (there, slot_there) in pairs[0] and cut == cuts[0]:
+            number = len(pairs)
         return pltpu.make_async_remote_copy(
-            src_ref=dens.at[r, slot],
-            dst_ref=dens.at[there, slot_there],
+            src_ref=dens.at[r, slot, :, :, cut],
+            dst_ref=dens.at[there, slot_there, :, :, cut],
             send_sem=send_sem.at[group_of],
-            recv_sem=recv_sem.at[numbers[there, slot_there]],
+            recv_sem=recv_sem.at[number],
             device_id=target,
             device_id_type=MESH,
         )
 
-    def to_x(r):
-        return remote(r, 0, (r + HALF) % CHUNKS, 2, at_x, r)
-
-    def to_y(r):
-        return remote(r, 0, r, 4, at_y, r)
+    def to_x(r, cut=slice(None)):
+        return remote(r, 0, (r + HALF) % CHUNKS, 2, at_x, r, cut)
+
+    def to_y(r, cut=slice(None)):
+        return remote(r, 0, r, 4, at_y, r, cut)
 
     def to_core(r):
         return pltpu.make_async_remote_copy(
@@ -253,8 +257,8 @@
     def relay_x(r):
         return remote(r, 4, r + HALF, 6, at_x, r + HALF)
 
-    def share(r, slot):
-        return remote(r, slot, r, slot + 1, at_core, r)
+    def share(r, slot, cut=slice(None)):
+        return remote(r, slot, r, slot + 1, at_core, r, cut)
 
     def all_sent(r):
         pltpu.make_async_remote_copy(
@@ -278,6 +282,19 @@
             device_id_type=MESH,
         ).wait_recv()
 
+    def take_piece(piece):
+        landed = dens.at[0, 1]
+        pltpu.make_async_remote_copy(
+            src_ref=landed,
+            dst_ref=landed,
+            send_sem=send_sem.at[0],
+            recv_sem=recv_sem.at[0 if piece else len(pairs)],
+            device_id=at_core,
+            device_id_type=MESH,
+        ).wait_recv()
+        for r, slot in pairs[0]:
+            share(r, slot, cuts[piece]).start()
+
     def take(*blocks):
         arrived(*blocks)
         for r, slot in blocks:
@@ -288,20 +305,22 @@
             pl.semaphore_wait(ready.at[step - 1], layers)
             both_layers(ready.at[step])
 
-    def prepare(r, slots):
+    def prepare(r, slots, cut=slice(None)):
         for slot in slots:
-            minus[r, slot] = -dens[r, slot, 1]
+            minus[r, slot, :, cut] = -dens[r, slot, 1, :, cut]
 
     with jax.named_scope("bar"):
         pl.semaphore_wait(barrier, 3 + layers)
     with jax.named_scope("own"):
         pltpu.make_async_copy(dens.at[:, 0], dens.at[:, 0], own_sem).wait()
-    for r in first_own:
-        if r >= HALF:
-            to_x(r).start()
-        else:
-            to_y(r).start()
+    for cut in cuts:
+        to_x(HALF, cut).start()
+        to_y(0, cut).start()
+    for r in range(CHUNKS):
         to_core(r).start()
+    for r in range(1, HALF):
+        to_x(HALF + r).start()
+        to_y(r).start()
     for r in range(HALF):
         to_x(r).start()
 
@@ -322,18 +341,18 @@
     green[0] = real_part * inverse
     green[1] = -imag_part * inverse
 
-    def product(slots, chunks, n):
-        low = chunks[0] * width
-        depth = len(chunks) * width
+    def product(slots, chunks, n, cut=slice(None)):
+        low = chunks[0] * width + (cut.start or 0)
+        depth = (cut.stop - cut.start) if cut.stop else len(chunks) * width
         left = []
         for plane in range(2):
             for r in chunks:
                 pieces = []
                 for slot in slots:
                     if plane == 0:
-                        pieces += [dens[r, slot, 0], minus[r, slot]]
+                        pieces += [dens[r, slot, 0, :, cut], minus[r, slot, :, cut]]
                     else:
-                        pieces += [dens[r, slot, 1], dens[r, slot, 0]]
+                        pieces += [dens[r, slot, 1, :, cut], dens[r, slot, 0, :, cut]]
                 left.append(jnp.concatenate(pieces, axis=0))
         right = [panel[n, plane, low : low + depth, :] for plane in range(2)]
         return lax.dot_general(
@@ -363,9 +382,12 @@
     def parts_of(value, slots):
         return [(slot, value[2 * i * rows : 2 * (i + 1) * rows]) for i, slot in enumerate(slots)]
 
-    def first_part(slots, n):
-        for slot, value in parts_of(product(slots, [0], n), slots):
-            acc[n, slot] = value
+    def first_part(slots, n, cut=slice(None)):
+        for slot, value in parts_of(product(slots, [0], n, cut), slots):
+            if cut.start:
+                acc[n, slot] += value
+            else:
+                acc[n, slot] = value
 
     def last_part(slots, n):
         for slot, value in parts_of(product(slots, [1], n), slots):
@@ -413,16 +435,25 @@
             done = until
 
     own_block(0)
-    for n in range(1, half):
-        own_block(n)
-        settle(own, n - 1)
+    own_block(1)
+    settle(own, 0)
+    own_block(2)
+    settle(own, 1)
+    with jax.named_scope("piece"):
+        take_piece(0)
+    prepare(0, direct, cuts[0])
+    for n in range(3):
+        first_part(direct, n, cuts[0])
+    own_block(3)
+    settle(own, 2)
     with jax.named_scope("take0"):
-        take((0, 2), (0, 4))
+        take_piece(1)
         onward_y(0).start()
         relay_x(0).start()
-    prepare(0, direct)
+    prepare(0, direct, cuts[1])
     for n in range(3):
-        first_part(direct, n)
+        first_part(direct, n, cuts[1])
+    first_part(direct, 3)
     settle(own, 3)
     own_block(4)
     with jax.named_scope("got0"):
@@ -430,9 +461,9 @@
     prepare(0, shared)
     first_part(shared, 0)
     settle(own, 4)
-    first_part(shared, 1)
-    first_part(shared, 2)
-    first_part(near, 3)
+    for n in range(1, half):
+        first_part(shared, n)
+    first_part(near, 4)
     with jax.named_scope("take1"):
         take((1, 2), (1, 4))
         onward_y(1).start()
@@ -441,7 +472,6 @@
             to_y(r).start()
         panel_copy(5).wait()
         panel_copy(6).wait()
-    first_part(near, 4)
     first_part(own + near, 5)
     first_part(own + near, 6)
     prepare(1, direct)
@@ -464,30 +494,30 @@
     prepare(0, far)
     for n in range(PANELS):
         first_part(far, n)
+    steps = [(pair, n) for n in (5, 6, 7) for pair in (own, xs, ys)]
+    finish(steps[:3], [(own, 5)])
     with jax.named_scope("take4"):
         take((2, 4), (2, 6))
+    finish(steps[3:], [(own, 6), (own, 7)])
+    with jax.named_scope("take5"):
+        take((3, 4), (3, 6))
         arrived((1, 7),)
         arrived((2, 3), (3, 3))
+        arrived((2, 5), (2, 7))
+        pass_ready(1)
     prepare(1, far)
     steps = [(far, n) for n in range(PANELS)]
-    finish(steps[:1], [])
-    finish(steps[1:], [(xs, 4)] + steps[:4])
-    with jax.named_scope("take5"):
-        arrived((2, 5), (2, 7))
-        take((3, 4), (3, 6))
-        pass_ready(1)
-    steps = [(pair, n) for n in (5, 6) for pair in (own, xs, ys)]
-    finish(steps[:1], [(ys, 4)])
-    finish(steps[1:], [(far, 4), steps[0], (far, 5), steps[1], steps[2], steps[3]])
+    finish(steps[:1], [(xs, 4)])
+    late_steps = [(ys, 4), (far, 0), (xs, 5), (far, 1), (ys, 5), (far, 2), (xs, 6), (far, 3), (xs, 7)]
+    finish(steps[1:5], late_steps)
     with jax.named_scope("last3"):
         arrived((3, 5), (3, 7))
         for step in range(2, count_pb - 1):
             pass_ready(step)
-    finish([(own, 7), (xs, 7)], [(xs, 6), (ys, 6), (own, 7), (far, 6)])
-    finish([(ys, 7)], [(far, 7), (xs, 7)])
-    early = spectra((0, 1, 2, 3, 6, 7))
-    settle(ys, 7)
-    late = spectra((4, 5))
+    finish(steps[5:], [(far, 4), (ys, 6), (far, 5), (ys, 7), (far, 6)])
+    early = spectra(range(6))
+    settle(far, 7)
+    late = spectra(far)
     parts[0, 0:1] = -jnp.sum(early[1] + late[1], axis=0, keepdims=True)
     parts[0, 1:2] = jnp.sum(early[0] + late[0], axis=0, keepdims=True)
     with jax.named_scope("ready"):
@@ -576,7 +606,7 @@
             pltpu.SemaphoreType.DMA((PANELS,)),
             pltpu.SemaphoreType.DMA((5,)),
             pltpu.SemaphoreType.DMA((CHUNKS,)),
-            pltpu.SemaphoreType.DMA((13,)),
+            pltpu.SemaphoreType.DMA((14,)),
             pltpu.SemaphoreType.DMA,
             pltpu.SemaphoreType.DMA,
             pltpu.SemaphoreType.DMA,

time: 34.2 us -> 34 us (level)
  no operation moved by 1% of the time
where the time goes in v3:
time: 34 us; the launch traced here: 33.9 us
  Pallas kernels  33.3 us (98%)
  local copies, waits for them, and re-layouts  0.56 us (2%)
    pallas_call x1, Pallas kernels, fused_body(): pl.pallas_call(functools.partial(fused_kernel, shape), out_shape=jax.Shap...  33.3 us

profile of v3, /device:TPU:0, one launch (start us, length us, event | category | flops | bytes accessed | tf_op | source)
XLA Modules:
  0.0 33.9 jit_solution(8083462343706591762)
XLA Ops:
  0.0 33.3 %shard_map.73 = f32[2,1,4]{2,1,0:T(1,128)S(1)} custom-call(bf16[1,2,32,4096]{3,2,1,0:T(8,128)(2,1)} %dens_hbm.1, bf16[1,1,2,2048,4096]{4,3,2,1,0:T(8,128)(2,1)} %screen_hbm.1, f32[16,256]{1,0:T(8,128)} %energy_hbm.1, s32[16]{0:T(128)} %filled_hbm.1, s32[4]{0:T(128)} %kmq_hbm.1, s32[4]{0:T(128)} %offset_hbm.1, f32[4]{0:T(128)} %weight_hbm.1), custom_call_target="tpu_custom_call" | custom-call | tf_op jit(solution)/shard_map/pallas_call | solution.py:587
  33.3 0.6 %copy.9 = f32[2,1,4]{2,1,0:T(1,128)} copy(f32[2,1,4]{2,1,0:T(1,128)S(1)} %shard_map.73) | data formatting | bytes 64
